TPU v7x, 8 devices: a whole 2x2x1 slice. The times are simulated.
8 devices in a mesh: data: 1 (over z), col: 2 (over y), row: 4 (over x, core).
Axes of the slice: x: 2, y: 2, z: 1, core: 2. Of those that a mesh axis runs over, the one named last changes fastest.
Arguments:
- residual: bfloat16 [128, 3072], P('data', 'row')
- gain_mlp: float32 [3072], P('row')
- gain_attn: float32 [3072], P('row')
- w_gate: bfloat16 [3072, 24576], P(None, ('col', 'row'))
- w_up: bfloat16 [3072, 24576], P(None, ('col', 'row'))
- w_down: bfloat16 [24576, 3072], P('col', 'row')
- w_qkv: bfloat16 [3072, 12288], P(None, ('col', 'row'))
Outputs:
- output 1: bfloat16 [128, 3072], P('data', 'row')
- output 2: bfloat16 [128, 12288], P('data', ('col', 'row'))
All inputs are finite; a program needn't handle non-finite values.
Results may differ from a plain program's by a relative error of at most 0.00415185.
Values are sent between devices in bfloat16 or wider.
A program may use at most 1 GiB of HBM per device.

v0:
```python
import jax
import jax.numpy as jnp
from jax import lax
from jax.sharding import PartitionSpec as P

NORM_EPS = 1e-6


def solution(mesh):
    row_size = mesh.shape['row']
    tok_spec = P('data', 'row')
    gain_spec = P('row')
    wide_spec = P(None, ('col', 'row'))
    down_spec = P('col', 'row')
    qkv_spec = P('data', ('col', 'row'))

    def shard_norm(shard, gain):
        shard_f = shard.astype(jnp.float32)
        sq_part = jnp.sum(shard_f * shard_f, axis=1, keepdims=True)
        sq_total = lax.psum(sq_part, 'row')
        row_scale = lax.rsqrt(sq_total / (shard.shape[1] * row_size) + NORM_EPS)
        return (shard_f * row_scale * gain).astype(jnp.bfloat16)

    def per_device(residual, gain_mlp, gain_attn, w_gate, w_up, w_down, w_qkv):
        normed = shard_norm(residual, gain_mlp)
        normed_full = lax.all_gather(normed, 'row', axis=1, tiled=True)
        gate_val = jnp.dot(normed_full, w_gate, preferred_element_type=jnp.float32)
        up_val = jnp.dot(normed_full, w_up, preferred_element_type=jnp.float32)
        act_val = (jax.nn.silu(gate_val) * up_val).astype(jnp.bfloat16)
        act_block = lax.all_gather(act_val, 'row', axis=1, tiled=True)
        down_part = jnp.dot(act_block, w_down, preferred_element_type=jnp.float32)
        down_sum = lax.psum(down_part, 'col')
        resid_next = (residual.astype(jnp.float32) + down_sum).astype(jnp.bfloat16)
        normed_next = shard_norm(resid_next, gain_attn)
        next_full = lax.all_gather(normed_next, 'row', axis=1, tiled=True)
        qkv_out = jnp.dot(next_full, w_qkv, preferred_element_type=jnp.float32).astype(jnp.bfloat16)
        return resid_next, qkv_out

    return jax.shard_map(per_device, mesh=mesh, in_specs=(tok_spec, gain_spec, gain_spec, wide_spec, wide_spec, down_spec, wide_spec), out_specs=(tok_spec, qkv_spec), check_vma=False)
```

profile of v0, /device:TPU:0, one launch (start us, length us, event | category | flops | bytes accessed | tf_op | source)
XLA Modules:
  0.0 132.5 jit_solution(3342734458487950415)
XLA Ops:
  7.2 0.0 all-gather.2.cloned.1.call-start
  7.2 1.0 fusion.4
  8.3 8.7 %psum.21 = f32[128,1]{0,1:T(1,128)S(1)} all-reduce(f32[128,1]{0,1:T(1,128)S(1)} %bitcast.14), channel_id=1, replica_groups=mesh['data'=1,'col'=2,'row'=4] {'row'}, use_global_device_ids=true, to_apply=%region_1.0 | all-reduce | flops 128 | bytes 1024 | tf_op jit(solution)/shard_map/psum | solution.py:20
  17.0 1.0 fusion.6
  18.1 10.8 %all_gather.9 = bf16[128,3072]{1,0:T(8,128)(2,1)S(1)} all-gather(bf16[128,768]{1,0:T(8,128)(2,1)S(1)} %fusion.6), channel_id=1, replica_groups=mesh['data'=1,'col'=2,'row'=4] {'row'}, dimensions={1}, use_global_device_ids=true | all-gather | bytes 983040 | tf_op jit(solution)/shard_map/all_gather | solution.py:26
  28.9 0.0 copy-start.3
  28.9 8.0 %fusion.9 = f32[128,3072]{1,0:T(8,128)S(1)} fusion(bf16[128,3072]{1,0:T(8,128)(2,1)S(1)} %all_gather.9, bf16[3072,3072]{1,0:T(8,128)(2,1)} %param.10), kind=kOutput, calls=%fused_computation.17 | convolution fusion | flops 2415919104 | bytes 21233664 | tf_op jit(solution)/shard_map/dot_general | solution.py:27
  36.8 3.8 %copy-done.3 = bf16[3072,3072]{1,0:T(8,128)(2,1)S(1)} copy-done((bf16[3072,3072]{1,0:T(8,128)(2,1)S(1)}, bf16[3072,3072]{1,0:T(8,128)(2,1)}, u32[]{:S(2)}) %copy-start.3) | copy-done | bytes 18874392
  40.6 4.0 %fusion = bf16[128,3072]{1,0:T(8,128)(2,1)} fusion(bf16[128,3072]{1,0:T(8,128)(2,1)S(1)} %all_gather.9, bf16[3072,3072]{1,0:T(8,128)(2,1)S(1)} %copy-done.3, f32[128,3072]{1,0:T(8,128)S(1)} %fusion.9), kind=kOutput, calls=%fused_computation.1 | convolution fusion | flops 2418278400 | bytes 22020096 | tf_op jit(solution)/shard_map/dot_general | solution.py:28
  44.6 0.0 all-gather.2.cloned.1.call-update
  44.7 0.0 copy-start
  44.7 0.0 copy-start.2
  44.7 0.0 all-reduce.2.cloned.1.call-start
  44.7 25.5 %all-gather.2.cloned.1.call-done = bf16[128,12288]{1,0:T(8,128)(2,1)} async-done(((bf16[128,3072]{1,0:T(8,128)(2,1)}), bf16[128,12288]{1,0:T(8,128)(2,1)}) %all-gather.2.cloned.1.call-update) | async-done | bytes 3145744 | tf_op jit(solution)/shard_map/all_gather | solution.py:30
  70.2 10.7 %fusion.10 = f32[128,768]{1,0:T(8,128)} fusion(bf16[128,12288]{1,0:T(8,128)(2,1)} %all-gather.2.cloned.1.call-done, bf16[12288,768]{1,0:T(8,128)(2,1)} %param.12), kind=kOutput, calls=%fused_computation.18 | convolution fusion | flops 2415919104 | bytes 22413312 | tf_op jit(solution)/shard_map/dot_general | solution.py:31
  80.9 0.0 all-reduce.2.cloned.1.call-update
  80.9 20.1 %all-reduce.2.cloned.1.call-done = f32[128,768]{1,0:T(8,128)} async-done(((f32[128,768]{1,0:T(8,128)}), f32[128,768]{1,0:T(8,128)}) %all-reduce.2.cloned.1.call-update) | async-done | bytes 393232 | tf_op jit(solution)/shard_map/psum | solution.py:32
  101.1 0.0 copy-done
  101.1 1.1 fusion.1
  102.2 0.0 copy-start.1
  102.2 6.9 %psum.23 = f32[128,1]{0,1:T(1,128)S(1)} all-reduce(f32[128,1]{0,1:T(1,128)S(1)} %bitcast.15), channel_id=1, replica_groups=mesh['data'=1,'col'=2,'row'=4] {'row'}, use_global_device_ids=true, to_apply=%region_4.5 | all-reduce | flops 128 | bytes 1024 | tf_op jit(solution)/shard_map/psum | solution.py:20
  109.1 0.0 copy-done.2
  109.1 0.1 fusion.3
  109.2 10.6 %all_gather.11 = bf16[128,3072]{1,0:T(8,128)(2,1)S(1)} all-gather(bf16[128,768]{1,0:T(8,128)(2,1)S(1)} %fusion.3), channel_id=1, replica_groups=mesh['data'=1,'col'=2,'row'=4] {'row'}, dimensions={1}, use_global_device_ids=true | all-gather | bytes 983040 | tf_op jit(solution)/shard_map/all_gather | solution.py:35
  119.8 5.8 %convolution_convert_fusion = bf16[128,1536]{1,0:T(8,128)(2,1)} fusion(bf16[128,3072]{1,0:T(8,128)(2,1)S(1)} %all_gather.11, bf16[3072,1536]{1,0:T(8,128)(2,1)} %param.13), kind=kOutput, calls=%fused_computation.2 | convolution fusion | flops 1208156160 | bytes 10616832 | tf_op jit(solution)/shard_map/dot_general | solution.py:36
  125.7 0.0 copy-done.1
  (2 shorter events, 0.0 us)
Async XLA Ops:
  7.2 63.1 %all-gather.2.cloned.1.call-start = ((), (), s32[]{:S(2)}) async-start(), calls=%async_computation | async-start | bytes 3932160 | tf_op jit(solution)/shard_map/all_gather | solution.py:30
  28.9 11.7 %copy-start.3 = (bf16[3072,3072]{1,0:T(8,128)(2,1)S(1)}, bf16[3072,3072]{1,0:T(8,128)(2,1)}, u32[]{:S(2)}) copy-start(bf16[3072,3072]{1,0:T(8,128)(2,1)} %param.11) | copy-start | bytes 56623108
  44.7 56.4 %copy-start = (bf16[128,768]{1,0:T(8,128)(2,1)S(1)}, bf16[128,768]{1,0:T(8,128)(2,1)}, u32[]{:S(2)}) copy-start(bf16[128,768]{1,0:T(8,128)(2,1)} %param.7) | copy-start | bytes 589828
  44.7 64.4 %copy-start.2 = (f32[768]{0:T(1024)S(1)}, f32[768]{0:T(1024)}, u32[]{:S(2)}) copy-start(f32[768]{0:T(1024)} %param.9) | copy-start | bytes 9220
  44.7 56.4 %all-reduce.2.cloned.1.call-start = ((), (), s32[]{:S(2)}) async-start(), calls=%async_computation.1 | async-start | bytes 786432 | tf_op jit(solution)/shard_map/psum | solution.py:32
  102.2 23.5 %copy-start.1 = (bf16[128,768]{1,0:T(8,128)(2,1)}, bf16[128,768]{1,0:T(8,128)(2,1)S(1)}, u32[]{:S(2)}) copy-start(bf16[128,768]{1,0:T(8,128)(2,1)S(1)} %get-tuple-element.3) | copy-start | bytes 589828
Sparse Core Ops, SparseCore 0:
  44.8 25.3 all-gather.1
  81.0 19.9 all-reduce.1
where the time goes:
time: 133 us
  waiting for transfers between devices  45.6 us (34%)
  blocking collectives  37.1 us (28%)
  matrix products  28.5 us (21%)
  between operations  14.1 us (11%)
  local copies, waits for them, and re-layouts  3.8 us (3%)
  other arithmetic  3.36 us (3%)
    all_gather x1, waiting for transfers between devices, per_device(): act_block = lax.all_gather(act_val, 'row', axis=1, tiled=True)  25.5 us
    psum x1, waiting for transfers between devices, per_device(): down_sum = lax.psum(down_part, 'col')  20.1 us
    psum x2, blocking collectives, shard_norm(): sq_total = lax.psum(sq_part, 'row')  15.6 us
    all_gather x1, blocking collectives, per_device(): normed_full = lax.all_gather(normed, 'row', axis=1, tiled=True)  10.8 us
    dot_general x1, matrix products, per_device(): down_part = jnp.dot(act_block, w_down, preferred_element_type=jnp.float32)  10.7 us
    all_gather x1, blocking collectives, per_device(): next_full = lax.all_gather(normed_next, 'row', axis=1, tiled=True)  10.6 us
    dot_general x1, matrix products, per_device(): gate_val = jnp.dot(normed_full, w_gate, preferred_element_type=jnp.float32)  7.95 us
    dot_general x1, matrix products, per_device(): jnp.dot(next_full, w_qkv, preferred_element_type=jnp.float32)  5.85 us
  transfers between devices with their start and end apart: 2, of which 2 were waited for; matrix products, arithmetic and copies ran while one was open for 0% of the time, Pallas kernels for 0%

commit v1 on v0

v1 whole, which is shorter than its diff:
```python
import functools

import jax
import jax.numpy as jnp
from jax import lax
from jax.experimental import pallas as pl
from jax.experimental.pallas import tpu as pltpu
from jax.sharding import PartitionSpec as P

NORM_EPS = 1e-6
MESH = pl.DeviceIdType.MESH
F32 = jnp.float32
BF16 = jnp.bfloat16

CB = 256
PASSES = ((0, 64), (64, 64))
GROUPS = ((0, 64), (64, 32), (96, 32))
AHEAD = 8


def kernel(res_h, g1_h, g2_h, wg_h, wu_h, wd_h, wq_h, xo, qo,
           wgu, wdb, abuf, xbuf, xpbuf, nbuf, acc, ybuf, gbuf,
           lsem, wsem, wdsem, wqsem, xs, xr, gs, gr, as_, ar, ys, yr, ps, pr):
    row, col = lax.axis_index('row'), lax.axis_index('col')
    mate = row + 1 - 2 * lax.rem(row, 2)
    near = lax.rem(row + 2, 4)
    far = lax.rem(mate + 2, 4)
    d_ff = wg_h.shape[1]
    chunks = d_ff // CB
    hid = res_h.shape[1]
    d_model = 4 * hid
    q_slabs = wq_h.shape[1] // CB

    def remote(src, dst, send, recv, device):
        return pltpu.make_async_remote_copy(src_ref=src, dst_ref=dst, send_sem=send, recv_sem=recv,
                                            device_id=device, device_id_type=MESH)

    def push(at, send, recv, kind):
        slot = (row, row, near)[kind]
        return remote(at(slot), at(slot), send(kind), recv(kind), {'row': (near, mate, mate)[kind]})

    def arrived(at, send, recv, kind):
        slot = (near, mate, far)[kind]
        remote(at(slot), at(slot), send(kind), recv(kind), {'row': mate}).wait_recv()

    def x_ex(p):
        t0, m = PASSES[p]
        return (lambda s: xbuf.at[s, pl.ds(t0, m)]), (lambda k: xs.at[p, k]), (lambda k: xr.at[p, k])

    g_ex = (lambda s: gbuf.at[s]), (lambda k: gs.at[k]), (lambda k: gr.at[k])

    def a_ex(g, j):
        t0, m = GROUPS[g]
        return (lambda s: abuf.at[j, s, pl.ds(t0, m)]), (lambda k: as_.at[g, j, k]), (lambda k: ar.at[g, j, k])

    def p_ex(g):
        t0, m = GROUPS[g]
        return (lambda s: xpbuf.at[s, pl.ds(t0, m)]), (lambda k: ps.at[g, k]), (lambda k: pr.at[g, k])

    def y_copy(g):
        rows = pl.ds(*GROUPS[g])
        return remote(acc.at[rows], ybuf.at[rows], ys.at[g], yr.at[g], {'col': 1 - col})

    def w_copy(j, half):
        src = (wg_h, wu_h)[half]
        start = j * CB if isinstance(j, int) else pl.multiple_of(j * CB, CB)
        return pltpu.make_async_copy(src.at[:, pl.ds(start, CB)], wgu.at[j, half], wsem.at[j, half])

    def wd_copy(j, s):
        start = pl.multiple_of(s * d_ff + j * CB, CB)
        return pltpu.make_async_copy(wd_h.at[pl.ds(start, CB)], wdb.at[j, pl.ds(s * CB, CB)], wdsem.at[j, s])

    def wq_copy(j):
        return pltpu.make_async_copy(wq_h.at[:, pl.ds(pl.multiple_of(j * CB, CB), CB)], wgu.at[j, 0], wqsem.at[j])

    loads = [pltpu.make_async_copy(res_h, xbuf.at[row], lsem.at[0]),
             pltpu.make_async_copy(g1_h, gbuf.at[row, 0], lsem.at[1]),
             pltpu.make_async_copy(g2_h, gbuf.at[row, 1], lsem.at[2])]
    for copy in loads:
        copy.start()
    for j in range(AHEAD):
        w_copy(j, 0).start()
        w_copy(j, 1).start()

    barrier = pltpu.get_barrier_semaphore()
    for device in ({'row': mate}, {'row': near}, {'col': 1 - col}):
        pl.semaphore_signal(barrier, inc=1, device_id=device, device_id_type=MESH)
    pl.semaphore_wait(barrier, 3)

    for copy in loads:
        copy.wait()
    push(*x_ex(0), 0).start()
    push(*g_ex, 0).start()
    push(*x_ex(0), 1).start()
    push(*g_ex, 1).start()
    push(*x_ex(1), 0).start()
    push(*x_ex(1), 1).start()
    acc[...] = jnp.zeros_like(acc)

    def normalise(src, which, t0, m):
        step = 16
        scales = []
        for t in range(t0, t0 + m, step):
            total = jnp.zeros((step, hid), F32)
            for q in range(4):
                v = src[q, t:t + step, :].astype(F32)
                total = total + v * v
            scales.append(lax.rsqrt(jnp.sum(total, axis=1, keepdims=True) / d_model + NORM_EPS))
        for i, t in enumerate(range(t0, t0 + m, step)):
            for q in range(4):
                v = src[q, t:t + step, :].astype(F32)
                nbuf[t:t + step, q * hid:(q + 1) * hid] = (v * scales[i] * gbuf[q, which:which + 1, :]).astype(BF16)

    arrived(*g_ex, 0)
    push(*g_ex, 2).start()
    arrived(*x_ex(0), 0)
    push(*x_ex(0), 2).start()
    for kind in (1, 2):
        arrived(*g_ex, kind)
        arrived(*x_ex(0), kind)
    normalise(xbuf, 0, *PASSES[0])

    def gate_up(p, j):
        t0, m = PASSES[p]
        n = nbuf[t0:t0 + m, :]
        gate = jnp.dot(n, wgu[j, 0], preferred_element_type=F32)
        up = jnp.dot(n, wgu[j, 1], preferred_element_type=F32)
        abuf[j, row, t0:t0 + m, :] = (jax.nn.silu(gate) * up).astype(BF16)

    def relay(g, j):
        arrived(*a_ex(g, j), 0)
        push(*a_ex(g, j), 2).start()

    def down_wait(g, j, first):
        arrived(*a_ex(g, j), 1)
        arrived(*a_ex(g, j), 2)
        if first:
            for s in range(4):
                wd_copy(j, s).wait()

    def down(g, j, n=1):
        t0, m = GROUPS[g]
        a = jnp.concatenate([abuf[j + i, s, t0:t0 + m, :] for i in range(n) for s in range(4)], axis=1)
        w = wdb[pl.ds(j, n)].reshape(n * 4 * CB, hid)
        acc[t0:t0 + m, :] += jnp.dot(a, w, preferred_element_type=F32)

    def first_pass(j, carry):
        @pl.when(j + AHEAD < chunks)
        def _():
            w_copy(j + AHEAD, 0).start()
            w_copy(j + AHEAD, 1).start()

        @pl.when(j == chunks - AHEAD)
        def _():
            def issue(i, c):
                for s in range(4):
                    wd_copy(i, s).start()
                return c
            lax.fori_loop(0, chunks, issue, 0)
            arrived(*x_ex(1), 0)
            push(*x_ex(1), 2).start()

        w_copy(j, 0).wait()
        w_copy(j, 1).wait()
        gate_up(0, j)
        push(*a_ex(0, j), 0).start()
        push(*a_ex(0, j), 1).start()
        return carry

    lax.fori_loop(0, chunks, first_pass, 0)

    arrived(*x_ex(1), 1)
    arrived(*x_ex(1), 2)
    normalise(xbuf, 0, *PASSES[1])

    def second_pass(j, with_down):
        relay(0, j)
        if with_down:
            down_wait(0, j - 1, True)
        gate_up(1, j)
        if with_down:
            down(0, j - 1)
        push(*a_ex(1, j), 0).start()
        push(*a_ex(1, j), 1).start()

    def second_pass_step(j, carry):
        second_pass(j, True)

        @pl.when(j < q_slabs)
        def _():
            wq_copy(j).start()
        return carry

    second_pass(0, False)
    wq_copy(0).start()
    lax.fori_loop(1, chunks, second_pass_step, 0)

    def late_push(j, carry):
        push(*a_ex(2, j), 0).start()
        push(*a_ex(2, j), 1).start()
        return carry

    lax.fori_loop(0, chunks, late_push, 0)
    down_wait(0, chunks - 1, True)
    down(0, chunks - 1)
    y_copy(0).start()

    def relays(g, lo, hi):
        def step(j, carry):
            relay(g, j)
            return carry
        lax.fori_loop(lo, hi, step, 0)

    def downs(g, lo, hi, n):
        def step(b, carry):
            j = lo + b * n
            for i in range(n):
                down_wait(g, j + i, False)
            down(g, j, n)
            return carry
        lax.fori_loop(0, (hi - lo) // n, step, 0)

    def residual(g):
        y_copy(g).wait_recv()
        t0, m = GROUPS[g]
        for t in range(t0, t0 + m, 16):
            rows = slice(t, t + 16)
            v = (xbuf[row, rows, :].astype(F32) + (acc[rows, :] + ybuf[rows, :])).astype(BF16)
            xpbuf[row, rows, :] = v
            xo[rows, :] = v
        push(*p_ex(g), 0).start()
        push(*p_ex(g), 1).start()

    def residual_relay(g):
        arrived(*p_ex(g), 0)
        push(*p_ex(g), 2).start()

    def qkv(groups):
        for g in groups:
            arrived(*p_ex(g), 1)
            arrived(*p_ex(g), 2)
            normalise(xpbuf, 1, *GROUPS[g])
        t0 = GROUPS[groups[0]][0]
        m = sum(GROUPS[g][1] for g in groups)

        def step(i, carry):
            n = nbuf[t0:t0 + m, :]
            for s in range(2):
                j = 2 * i + s
                out = jnp.dot(n, wgu[j, 0], preferred_element_type=F32)
                qo[t0:t0 + m, pl.ds(pl.multiple_of(j * CB, CB), CB)] = out.astype(BF16)
            return carry
        lax.fori_loop(0, q_slabs // 2, step, 0)

    relays(1, 0, chunks)
    downs(1, 0, chunks, 4)
    y_copy(1).start()

    half = chunks // 2
    relays(2, 0, half)
    downs(2, 0, half, 2)
    residual(0)
    relays(2, half, chunks)
    downs(2, half, chunks, 2)
    y_copy(2).start()

    residual_relay(0)
    residual(1)

    def drain(j, carry):
        for g in range(3):
            for kind in range(3):
                push(*a_ex(g, j), kind).wait_send()
        return carry
    lax.fori_loop(0, chunks, drain, 0)
    for kind in range(3):
        push(*g_ex, kind).wait_send()
        for p in range(2):
            push(*x_ex(p), kind).wait_send()
    for j in range(q_slabs):
        wq_copy(j).wait()

    residual_relay(1)
    residual(2)
    qkv((0, 1))
    residual_relay(2)
    qkv((2,))
    for g in range(3):
        y_copy(g).wait_send()
        for kind in range(3):
            push(*p_ex(g), kind).wait_send()


def solution(mesh):
    def per_device(residual, gain_mlp, gain_attn, w_gate, w_up, w_down, w_qkv):
        tokens, hid = residual.shape
        d_model, d_ff = w_gate.shape
        q_width = w_qkv.shape[1]
        chunks = d_ff // CB
        any_spec = pl.BlockSpec(memory_space=pl.ANY)
        vmem_spec = pl.BlockSpec(memory_space=pltpu.VMEM)
        dma = pltpu.SemaphoreType.DMA
        groups, passes = len(GROUPS), len(PASSES)
        return pl.pallas_call(
            kernel,
            name='block',
            out_shape=(jax.ShapeDtypeStruct((tokens, hid), BF16), jax.ShapeDtypeStruct((tokens, q_width), BF16)),
            in_specs=[any_spec] * 7,
            out_specs=(vmem_spec, vmem_spec),
            scratch_shapes=[
                pltpu.VMEM((chunks, 2, d_model, CB), BF16),
                pltpu.VMEM((chunks, 4 * CB, hid), BF16),
                pltpu.VMEM((chunks, 4, tokens, CB), BF16),
                pltpu.VMEM((4, tokens, hid), BF16),
                pltpu.VMEM((4, tokens, hid), BF16),
                pltpu.VMEM((tokens, d_model), BF16),
                pltpu.VMEM((tokens, hid), F32),
                pltpu.VMEM((tokens, hid), F32),
                pltpu.VMEM((4, 2, hid), F32),
                dma((3,)),
                dma((chunks, 2)),
                dma((chunks, 4)),
                dma((q_width // CB,)),
                dma((passes, 3)), dma((passes, 3)),
                dma((3,)), dma((3,)),
                dma((groups, chunks, 3)), dma((groups, chunks, 3)),
                dma((groups,)), dma((groups,)),
                dma((groups, 3)), dma((groups, 3)),
            ],
            compiler_params=pltpu.CompilerParams(collective_id=0, has_side_effects=True,
                                                 vmem_limit_bytes=67_043_328),
        )(residual, gain_mlp, gain_attn, w_gate, w_up, w_down, w_qkv)

    tok_spec, gain_spec = P('data', 'row'), P('row')
    wide_spec = P(None, ('col', 'row'))
    return jax.shard_map(
        per_device, mesh=mesh,
        in_specs=(tok_spec, gain_spec, gain_spec, wide_spec, wide_spec, P('col', 'row'), wide_spec),
        out_specs=(tok_spec, P('data', ('col', 'row'))), check_vma=False)
```

time: 133 us -> 68.6 us (0.52)
  Pallas kernels: 0 us -> 64.1 us
  waiting for transfers between devices: 45.6 us -> 0 us
  blocking collectives: 37.1 us -> 0 us
  matrix products: 28.5 us -> 0 us
  between operations: 14.1 us -> 0.64 us
  other arithmetic: 3.36 us -> 0 us
    pallas_call x0 -> x1, Pallas kernels: none -> 64.1 us  [per_device(): pl.pallas_call(kernel, name='block', out_shape=(jax.ShapeDtypeStruct((tok...]
    dot_general x4 -> x0, matrix products: 28.5 us -> none  [the longest x1 10.7 us: per_device(): down_part = jnp.dot(act_block, w_down, preferred_element_type=jnp.float32)]
    all_gather x1 -> x0, waiting for transfers between devices: 25.5 us -> none  [per_device(): act_block = lax.all_gather(act_val, 'row', axis=1, tiled=True)]
    all_gather x2 -> x0, blocking collectives: 21.4 us -> none  [the longest x1 10.8 us: per_device(): normed_full = lax.all_gather(normed, 'row', axis=1, tiled=True)]
    psum x1 -> x0, waiting for transfers between devices: 20.1 us -> none  [per_device(): down_sum = lax.psum(down_part, 'col')]
    psum x2 -> x0, blocking collectives: 15.6 us -> none  [shard_norm(): sq_total = lax.psum(sq_part, 'row')]
    reduce_sum x2 -> x0, other arithmetic: 2.18 us -> none  [shard_norm(): sq_part = jnp.sum(shard_f * shard_f, axis=1, keepdims=True)]
    unnamed x8 -> x2, local copies, waits for them, and re-layouts: 3.8 us -> 3.38 us
  transfers between devices with their start and end apart: 2 -> 0, of which waited for: 2 -> 0; matrix products, arithmetic and copies ran while one was open for 0% -> 0% of each run, Pallas kernels for 0% -> 0%
where the time goes in v1:
time: 68.6 us; the launch traced here: 68.1 us
  Pallas kernels  64.1 us (93%)
  local copies, waits for them, and re-layouts  3.38 us (5%)
    pallas_call x1, Pallas kernels, per_device(): pl.pallas_call(kernel, name='block', out_shape=(jax.ShapeDtypeStruct((tok...  64.1 us
    unnamed x2, local copies, waits for them, and re-layouts  3.38 us

profile of v1, /device:TPU:0, one launch (start us, length us, event | category | flops | bytes accessed | tf_op | source)
XLA Modules:
  0.0 68.1 jit_solution(7868212398272103891)
XLA Ops:
  0.6 64.1 %block.1 = (bf16[128,768]{1,0:T(8,128)(2,1)}, bf16[128,1536]{1,0:T(8,128)(2,1)}) custom-call(bf16[128,768]{1,0:T(8,128)(2,1)} %res_h.1, f32[768]{0:T(1024)} %g1_h.1, f32[768]{0:T(1024)} %g2_h.1, bf16[3072,3072]{1,0:T(8,128)(2,1)} %wg_h.1, bf16[3072,3072]{1,0:T(8,128)(2,1)} %wu_h.1, bf16[12288,768]{1,0:T(8,128)(2,1)} %wd_h.1, bf16[3072,1536]{1,0:T(8,128)(2,1)} %wq_h.1), custom_call_target="tpu_custom_call" | custom-call | tf_op jit(solution)/shard_map/block/pallas_call | solution.py:304
  64.7 1.6 %copy.11 = bf16[128,768]{1,0:T(8,128)(2,1)} copy(bf16[128,768]{1,0:T(8,128)(2,1)} %get-tuple-element.4) | data formatting | bytes 393216
  66.3 1.8 %copy.12 = bf16[128,1536]{1,0:T(8,128)(2,1)} copy(bf16[128,1536]{1,0:T(8,128)(2,1)} %get-tuple-element.5) | data formatting | bytes 786432
